TPU v7x, 256 devices: a whole 4x4x8 slice. The times are simulated.
256 devices in a mesh: fsdp: 32 (over z_hi, y, core), tensor: 8 (over z_lo, x).
Axes of the slice: x: 4, y: 4, z: 8 (z_hi: 4, z_lo: 2; z = z_hi * 2 + z_lo), core: 2. Of those that a mesh axis runs over, the one named last changes fastest.
Arguments:
- tokens: bfloat16 [4096, 8192], P('fsdp'), may hold values from -6 to 6
- cotangent: bfloat16 [4096, 8192], P('fsdp'), may hold values from -1.5 to 1.5
- gate_blocks: bfloat16 [8, 64, 128, 128], P('tensor', 'fsdp'), may hold values from -0.25 to 0.25
- up_blocks: bfloat16 [8, 64, 128, 128], P('tensor', 'fsdp'), may hold values from -0.25 to 0.25
- down_blocks: bfloat16 [8, 64, 128, 128], P('tensor', 'fsdp'), may hold values from -0.25 to 0.25
- gate_where: int32 [8, 64], P('tensor'), may hold values from 0 to 895, as said below
- up_where: int32 [8, 64], P('tensor'), may hold values from 0 to 895, as said below
- down_where: int32 [8, 64], P('tensor'), may hold values from 0 to 895, as said below
- block_counts: int32 [3, 8], P(None, 'tensor'), may hold values from 32 to 64, as said below
Outputs:
- outputs: bfloat16 [4096, 8192], P('fsdp', 'tensor')
- input_grads: bfloat16 [4096, 8192], P('fsdp', 'tensor')
- gate_grads: bfloat16 [8, 64, 128, 128], P('tensor', 'fsdp')
- up_grads: bfloat16 [8, 64, 128, 128], P('tensor', 'fsdp')
- down_grads: bfloat16 [8, 64, 128, 128], P('tensor', 'fsdp')
Inputs may be any that keep to these rules, and one draw needn't show every extreme that they name: Within one group of hidden units the 64 positions of gate_where are distinct. Within one group of hidden units the 64 positions of up_where are distinct. Within one group of hidden units the 64 positions of down_where are distinct. `block_counts`: for each matrix some group has all 64 slots live.
All inputs are finite; a program needn't handle non-finite values.
Results may differ from a plain program's by a relative error of at most 0.015.
Values may be sent and summed in bfloat16 or wider, within the bound.
A program may use at most 128 MiB of HBM per device.

v0:
```python
import jax
import jax.numpy as jnp
from jax import lax
from jax.sharding import PartitionSpec as P

FF = 14336


def blockwise(pattern, left_side, right_side):
    return jnp.einsum(pattern, left_side, right_side, preferred_element_type=jnp.float32)


def collect(block_terms, segment_ids, segments):
    return jax.ops.segment_sum(block_terms, segment_ids, num_segments=segments)


def shards(
    tokens,
    cotangent,
    gate_blocks,
    up_blocks,
    down_blocks,
    gate_where,
    up_where,
    down_where,
    block_counts,
):
    tok_rows, tok_width = tokens.shape
    row_blocks = tok_width // 128
    col_blocks = FF // (128 * lax.axis_size("tensor"))
    slot_count = gate_where.shape[1]
    rows_blocked = tokens.reshape(tok_rows, row_blocks, 128).transpose(1, 0, 2)
    grad_blocked = cotangent.reshape(tok_rows, row_blocks, 128).transpose(1, 0, 2)
    live_slots = lax.broadcasted_iota(jnp.int32, (3, slot_count), 1) < block_counts
    live_blocks = live_slots.astype(jnp.bfloat16)[:, :, None, None]
    live_parts = live_slots.astype(jnp.float32)[:, :, None, None]
    gate_all, up_all, down_all = (
        lax.all_gather(gate_blocks, "fsdp", axis=1, tiled=True),
        lax.all_gather(up_blocks, "fsdp", axis=1, tiled=True),
        lax.all_gather(down_blocks, "fsdp", axis=1, tiled=True),
    )
    gate_eff = gate_all[0] * live_blocks[0]
    up_eff = up_all[0] * live_blocks[1]
    gate_row = gate_where[0] // col_blocks
    gate_col = gate_where[0] % col_blocks
    up_row = up_where[0] // col_blocks
    up_col = up_where[0] % col_blocks
    down_ff = down_where[0] // row_blocks
    down_d = down_where[0] % row_blocks
    rows_gate = jnp.take(rows_blocked, gate_row, axis=0)
    rows_up = jnp.take(rows_blocked, up_row, axis=0)
    gate_val = collect(blockwise("ntk,nkj->ntj", rows_gate, gate_eff), gate_col, col_blocks)
    up_val = collect(blockwise("ntk,nkj->ntj", rows_up, up_eff), up_col, col_blocks)
    down_eff = down_all[0] * live_blocks[2]
    gate_sig = jax.nn.sigmoid(gate_val)
    silu_gate = gate_val * gate_sig
    hidden = (silu_gate * up_val).astype(jnp.bfloat16)
    hidden_sel = jnp.take(hidden, down_ff, axis=0)
    grad_sel = jnp.take(grad_blocked, down_d, axis=0)
    output_term = collect(blockwise("ntk,nkj->ntj", hidden_sel, down_eff), down_d, row_blocks)
    output_sum = lax.psum_scatter(
        output_term.astype(jnp.bfloat16), "tensor", scatter_dimension=0, tiled=True
    ).astype(jnp.float32)
    hidden_grad = collect(blockwise("ntj,nkj->ntk", grad_sel, down_eff), down_ff, col_blocks)
    down_part = blockwise("ntk,ntj->nkj", hidden_sel, grad_sel) * live_parts[2]
    gate_delta = (hidden_grad * up_val * gate_sig * (1.0 + gate_val * (1.0 - gate_sig))).astype(
        jnp.bfloat16
    )
    up_delta = (hidden_grad * silu_gate).astype(jnp.bfloat16)
    delta_gate = jnp.take(gate_delta, gate_col, axis=0)
    delta_up = jnp.take(up_delta, up_col, axis=0)
    input_term = collect(blockwise("ntj,nkj->ntk", delta_gate, gate_eff), gate_row, row_blocks)
    input_term = input_term + collect(
        blockwise("ntj,nkj->ntk", delta_up, up_eff), up_row, row_blocks
    )
    gate_part = blockwise("ntk,ntj->nkj", rows_gate, delta_gate) * live_parts[0]
    up_part = blockwise("ntk,ntj->nkj", rows_up, delta_up) * live_parts[1]
    gate_sum, up_sum, down_sum = (
        lax.psum_scatter(
            gate_part[None].astype(jnp.bfloat16), "fsdp", scatter_dimension=1, tiled=True
        ).astype(jnp.float32),
        lax.psum_scatter(
            up_part[None].astype(jnp.bfloat16), "fsdp", scatter_dimension=1, tiled=True
        ).astype(jnp.float32),
        lax.psum_scatter(
            down_part[None].astype(jnp.bfloat16), "fsdp", scatter_dimension=1, tiled=True
        ).astype(jnp.float32),
    )
    input_sum = lax.psum_scatter(
        input_term.astype(jnp.bfloat16), "tensor", scatter_dimension=0, tiled=True
    ).astype(jnp.float32)
    outputs = output_sum.transpose(1, 0, 2).reshape(tok_rows, -1).astype(jnp.bfloat16)
    input_grads = input_sum.transpose(1, 0, 2).reshape(tok_rows, -1).astype(jnp.bfloat16)
    return (
        outputs,
        input_grads,
        gate_sum.astype(jnp.bfloat16),
        up_sum.astype(jnp.bfloat16),
        down_sum.astype(jnp.bfloat16),
    )


def solution(mesh):
    placed = (
        P("fsdp", None),
        P("fsdp", None),
        P("tensor", "fsdp", None, None),
        P("tensor", "fsdp", None, None),
        P("tensor", "fsdp", None, None),
        P("tensor", None),
        P("tensor", None),
        P("tensor", None),
        P(None, "tensor"),
    )
    return jax.shard_map(
        shards,
        mesh=mesh,
        in_specs=placed,
        out_specs=(
            P("fsdp", "tensor"),
            P("fsdp", "tensor"),
            P("tensor", "fsdp", None, None),
            P("tensor", "fsdp", None, None),
            P("tensor", "fsdp", None, None),
        ),
        check_vma=False,
    )
```

profile of v0, /device:TPU:2, one launch (start us, length us, event | category | flops | bytes accessed | tf_op | source)
XLA Modules:
  0.0 606.7 jit_solution(10214975213814710242)
XLA Ops:
  7.2 0.0 all-gather.8.cloned.1.call-start
  7.2 0.7 all-gather.8.cloned.1.call-update
  7.9 0.0 all-gather.4.cloned.1.call-start
  7.9 0.7 all-gather.4.cloned.1.call-update
  8.6 0.0 all-gather.6.cloned.1.call-start
  8.7 0.7 all-gather.6.cloned.1.call-update
  9.4 0.0 reduce-scatter.6.cloned.1.call-start
  9.4 4.1 copy.31
  13.6 3.2 copy.32
  16.9 2.2 gather_fusion.1
  19.1 2.2 gather_fusion
  21.3 3.2 copy.37
  24.5 3.0 copy.38
  27.5 2.5 gather_fusion.3
  30.1 0.1 fusion.16
  30.2 38.1 %all-gather.8.cloned.1.call-done = bf16[1,64,128,128]{3,2,0,1:T(8,128)(2,1)} async-done(((bf16[1,2,128,128]{3,2,0,1:T(8,128)(2,1)}), bf16[1,64,128,128]{3,2,0,1:T(8,128)(2,1)}) %all-gather.8.cloned.1.call-update) | async-done | bytes 2097168 | tf_op jit(solution)/shard_map/all_gather | solution.py:40
  68.3 5.2 fusion.4
  73.5 0.1 broadcast.235.clone
  73.6 8.9 %scatter_fusion.3 = f32[14,128,128]{2,1,0:T(8,128)S(1)} fusion(f32[14,128,128]{2,1,0:T(8,128)S(1)} %broadcast.235.clone, s32[64]{0:T(128)S(1)} %get-tuple-element.50, f32[64,128,128]{2,1,0:T(8,128)} %fusion.4), kind=kCustom, calls=%fused_computation.9 | custom fusion | flops 1048576 | bytes 12583168 | tf_op jit(solution)/shard_map/scatter-add | solution.py:14
  82.5 40.1 %all-gather.4.cloned.1.call-done = bf16[1,64,128,128]{3,2,0,1:T(8,128)(2,1)} async-done(((bf16[1,2,128,128]{3,2,0,1:T(8,128)(2,1)}), bf16[1,64,128,128]{3,2,0,1:T(8,128)(2,1)}) %all-gather.4.cloned.1.call-update) | async-done | bytes 2097168 | tf_op jit(solution)/shard_map/all_gather | solution.py:38
  122.7 4.3 fusion.1
  127.0 0.1 broadcast.235.clone.1
  127.1 8.8 %scatter_fusion = f32[14,128,128]{2,1,0:T(8,128)S(1)} fusion(f32[14,128,128]{2,1,0:T(8,128)S(1)} %broadcast.235.clone.1, s32[64]{0:T(128)S(1)} %get-tuple-element.52, f32[64,128,128]{2,1,0:T(8,128)} %fusion.1), kind=kCustom, calls=%fused_computation.6 | custom fusion | flops 1048576 | bytes 12583168 | tf_op jit(solution)/shard_map/scatter-add | solution.py:14
  135.9 41.1 %all-gather.6.cloned.1.call-done = bf16[1,64,128,128]{3,2,0,1:T(8,128)(2,1)} async-done(((bf16[1,2,128,128]{3,2,0,1:T(8,128)(2,1)}), bf16[1,64,128,128]{3,2,0,1:T(8,128)(2,1)}) %all-gather.6.cloned.1.call-update) | async-done | bytes 2097168 | tf_op jit(solution)/shard_map/all_gather | solution.py:39
  177.0 5.0 fusion.3
  182.0 0.1 broadcast.235.clone.2
  182.0 8.8 %scatter_fusion.1 = f32[14,128,128]{2,1,0:T(8,128)S(1)} fusion(f32[14,128,128]{2,1,0:T(8,128)S(1)} %broadcast.235.clone.2, s32[64]{0:T(128)S(1)} %get-tuple-element.53, f32[64,128,128]{2,1,0:T(8,128)} %fusion.3), kind=kCustom, calls=%fused_computation.7 | custom fusion | flops 1048576 | bytes 12583168 | tf_op jit(solution)/shard_map/scatter-add | solution.py:14
  190.8 1.6 multiply_convert_fusion.3
  192.5 3.3 gather_fusion.2
  195.8 4.3 fusion.5
  200.1 2.5 broadcast.233.clone
  202.6 13.5 %scatter_fusion.2 = f32[64,128,128]{2,1,0:T(8,128)} fusion(f32[64,128,128]{2,1,0:T(8,128)} %broadcast.233.clone, s32[64]{0:T(128)S(1)} %get-tuple-element.51, f32[64,128,128]{2,1,0:T(8,128)} %fusion.5), kind=kCustom, calls=%fused_computation.8 | custom fusion | flops 1048576 | bytes 12583168 | tf_op jit(solution)/shard_map/scatter-add | solution.py:14
  216.1 3.9 convert_element_type.63
  220.1 0.0 reduce-scatter.6.cloned.1.call-update
  220.1 0.2 reduce-scatter.8.cloned.1.call-start
  220.3 0.8 copy-done
  221.1 2.2 gather_fusion.5
  223.3 2.2 gather_fusion.4
  225.4 5.2 fusion
  230.6 2.5 broadcast.233.clone.1
  233.1 13.7 %scatter_fusion.4 = f32[64,128,128]{2,1,0:T(8,128)} fusion(f32[64,128,128]{2,1,0:T(8,128)} %broadcast.233.clone.1, s32[64]{0:T(128)S(1)} %get-tuple-element.25, f32[64,128,128]{2,1,0:T(8,128)} %fusion), kind=kCustom, calls=%fused_computation.10 | custom fusion | flops 1048576 | bytes 12583168 | tf_op jit(solution)/shard_map/scatter-add | solution.py:14
  246.8 5.2 fusion.2
  252.1 2.5 broadcast.233.clone.2
  254.5 13.6 %scatter_fusion.5 = f32[64,128,128]{2,1,0:T(8,128)} fusion(f32[64,128,128]{2,1,0:T(8,128)} %broadcast.233.clone.2, s32[64]{0:T(128)S(1)} %get-tuple-element.19, f32[64,128,128]{2,1,0:T(8,128)} %fusion.2), kind=kCustom, calls=%fused_computation.11 | custom fusion | flops 1048576 | bytes 12583168 | tf_op jit(solution)/shard_map/scatter-add | solution.py:14
  268.1 5.8 add_convert_fusion
  273.9 0.0 reduce-scatter.8.cloned.1.call-update
  273.9 0.0 reduce-scatter.12.cloned.1.call-start
  274.0 1.5 copy-done.4
  275.5 4.2 fusion.7
  279.7 0.0 reduce-scatter.10.cloned.1.call-start
  279.7 1.5 copy-done.8
  281.2 4.4 fusion.6
  285.6 0.0 reduce-scatter.14.cloned.1.call-start
  285.7 1.5 copy-done.6
  287.2 4.2 fusion.8
  291.4 0.0 reduce-scatter.6.cloned.1.call-done
  291.4 1.1 copy.36
  292.5 0.9 copy.43
  293.4 20.3 %reduce-scatter.8.cloned.1.call-done = bf16[8,128,128]{2,1,0:T(8,128)(2,1)} async-done(((bf16[64,128,128]{2,1,0:T(8,128)(2,1)}), bf16[8,128,128]{2,1,0:T(8,128)(2,1)}) %reduce-scatter.8.cloned.1.call-update) | async-done | bytes 262160 | tf_op jit(solution)/shard_map/reduce_scatter | solution.py:89
  313.7 1.1 copy.39
  314.8 0.9 copy.44
  315.7 95.9 %reduce-scatter.12.cloned.1.call-done = bf16[1,2,128,128]{3,2,1,0:T(8,128)(2,1)} async-done(((bf16[1,64,128,128]{3,2,1,0:T(8,128)(2,1)}), bf16[1,2,128,128]{3,2,1,0:T(8,128)(2,1)}) %reduce-scatter.12.cloned.1.call-update) | async-done | bytes 65552 | tf_op jit(solution)/shard_map/reduce_scatter | solution.py:82
  411.6 94.2 %reduce-scatter.10.cloned.1.call-done = bf16[1,2,128,128]{3,2,1,0:T(8,128)(2,1)} async-done(((bf16[1,64,128,128]{3,2,1,0:T(8,128)(2,1)}), bf16[1,2,128,128]{3,2,1,0:T(8,128)(2,1)}) %reduce-scatter.10.cloned.1.call-update) | async-done | bytes 65552 | tf_op jit(solution)/shard_map/reduce_scatter | solution.py:79
  505.8 94.1 %reduce-scatter.14.cloned.1.call-done = bf16[1,2,128,128]{3,2,1,0:T(8,128)(2,1)} async-done(((bf16[1,64,128,128]{3,2,1,0:T(8,128)(2,1)}), bf16[1,2,128,128]{3,2,1,0:T(8,128)(2,1)}) %reduce-scatter.14.cloned.1.call-update) | async-done | bytes 65552 | tf_op jit(solution)/shard_map/reduce_scatter | solution.py:85
  (36 shorter events, 0.2 us)
Async XLA Ops:
  7.2 61.1 %all-gather.8.cloned.1.call-start = ((), (), s32[]{:S(2)}) async-start(), calls=%async_computation.7 | async-start | bytes 2162688 | tf_op jit(solution)/shard_map/all_gather | solution.py:40
  7.9 114.8 %all-gather.4.cloned.1.call-start = ((), (), s32[]{:S(2)}) async-start(), calls=%async_computation.5 | async-start | bytes 2162688 | tf_op jit(solution)/shard_map/all_gather | solution.py:38
  8.6 168.3 %all-gather.6.cloned.1.call-start = ((), (), s32[]{:S(2)}) async-start(), calls=%async_computation.6 | async-start | bytes 2162688 | tf_op jit(solution)/shard_map/all_gather | solution.py:39
  9.4 282.0 %reduce-scatter.6.cloned.1.call-start = ((), (), s32[]{:S(2)}) async-start(), calls=%async_computation.8 | async-start | bytes 2359296 | tf_op jit(solution)/shard_map/reduce_scatter | solution.py:61
  13.6 3.2 copy-start.9
  16.9 2.2 copy-start.10
  24.5 3.0 copy-start.11
  27.5 2.6 copy-start.12
  30.1 43.4 %copy-start.5 = (bf16[64,128,128]{2,1,0:T(8,128)(2,1)}, bf16[64,128,128]{2,1,0:T(8,128)(2,1)S(1)}, u32[]{:S(2)}) copy-start(bf16[64,128,128]{2,1,0:T(8,128)(2,1)S(1)} %gather_fusion.3) | copy-start | bytes 6291460
  73.6 49.1 %copy-start.7 = (bf16[64,128,128]{2,1,0:T(8,128)(2,1)S(1)}, bf16[64,128,128]{2,1,0:T(8,128)(2,1)}, u32[]{:S(2)}) copy-start(bf16[64,128,128]{2,1,0:T(8,128)(2,1)} %gather_fusion) | copy-start | bytes 6291460
  192.5 3.3 copy-start.3
  220.0 1.0 copy-start
  220.1 93.6 %reduce-scatter.8.cloned.1.call-start = ((), (), s32[]{:S(2)}) async-start(), calls=%async_computation.9 | async-start | bytes 2359296 | tf_op jit(solution)/shard_map/reduce_scatter | solution.py:89
  223.3 2.2 copy-start.1
  233.1 13.7 %copy-start.2 = (bf16[1,64,128,128]{3,2,0,1:T(8,128)(2,1)S(1)}, bf16[1,64,128,128]{3,2,0,1:T(8,128)(2,1)}, u32[]{:S(2)}) copy-start(bf16[1,64,128,128]{3,2,0,1:T(8,128)(2,1)} %all-gather.6.cloned.1.call-done) | copy-start | bytes 6291460
  273.9 1.6 copy-start.4
  273.9 137.7 %reduce-scatter.12.cloned.1.call-start = ((), (), s32[]{:S(2)}) async-start(), calls=%async_computation.11 | async-start | bytes 2162688 | tf_op jit(solution)/shard_map/reduce_scatter | solution.py:82
  279.6 1.6 copy-start.8
  279.7 226.1 %reduce-scatter.10.cloned.1.call-start = ((), (), s32[]{:S(2)}) async-start(), calls=%async_computation.10 | async-start | bytes 2162688 | tf_op jit(solution)/shard_map/reduce_scatter | solution.py:79
  285.6 1.6 copy-start.6
  285.6 314.3 %reduce-scatter.14.cloned.1.call-start = ((), (), s32[]{:S(2)}) async-start(), calls=%async_computation.12 | async-start | bytes 2162688 | tf_op jit(solution)/shard_map/reduce_scatter | solution.py:85
Sparse Core Ops, SparseCore 0:
  10.5 57.7 all-gather.7
  70.9 51.7 all-gather.3
  125.2 51.7 all-gather.5
  220.2 39.8 reduce-scatter.5
  274.0 39.6 reduce-scatter.7
  318.0 93.5 reduce-scatter.11
  416.0 89.6 reduce-scatter.9
  510.2 89.6 reduce-scatter.13
where the time goes:
time: 608 us; the launch traced here: 607 us
  waiting for transfers between devices  426 us (70%)
  other arithmetic  78.8 us (13%)
  local copies, waits for them, and re-layouts  45.1 us (7%)
  matrix products  42 us (7%)
  between operations  14.4 us (2%)
    reduce_scatter x1, waiting for transfers between devices, shards(): lax.psum_scatter(up_part[None].astype(jnp.bfloat16), 'fsdp', scatter_dime...  95.9 us
    reduce_scatter x1, waiting for transfers between devices, shards(): lax.psum_scatter(gate_part[None].astype(jnp.bfloat16), 'fsdp', scatter_di...  94.2 us
    reduce_scatter x1, waiting for transfers between devices, shards(): lax.psum_scatter(down_part[None].astype(jnp.bfloat16), 'fsdp', scatter_di...  94.1 us
    scatter-add x6, other arithmetic, collect(): return jax.ops.segment_sum(block_terms, segment_ids, num_segments=segments)  67.3 us
    dot_general x9, matrix products, blockwise(): jnp.einsum(pattern, left_side, right_side, preferred_element_type=jnp.flo...  42 us
    all_gather x1, waiting for transfers between devices, shards(): lax.all_gather(up_blocks, 'fsdp', axis=1, tiled=True)  41.1 us
    all_gather x1, waiting for transfers between devices, shards(): lax.all_gather(gate_blocks, 'fsdp', axis=1, tiled=True)  40.1 us
    all_gather x1, waiting for transfers between devices, shards(): lax.all_gather(down_blocks, 'fsdp', axis=1, tiled=True)  38.1 us
  transfers between devices with their start and end apart: 8, of which 7 were waited for; matrix products, arithmetic and copies ran while one was open for 19% of the time, Pallas kernels for 0%

commit v1 on v0

--- a/solution.py
+++ b/solution.py
@@ -4,6 +4,11 @@
 from jax.sharding import PartitionSpec as P
 
 FF = 14336
+
+
+def gather_over(shard, name, dim):
+    outgoing = jnp.stack([shard] * lax.axis_size(name))
+    return jnp.concatenate(lax.all_to_all(outgoing, name, 0, 0), axis=dim)
 
 
 def blockwise(pattern, left_side, right_side):
@@ -37,7 +42,7 @@
     gate_all, up_all, down_all = (
         lax.all_gather(gate_blocks, "fsdp", axis=1, tiled=True),
         lax.all_gather(up_blocks, "fsdp", axis=1, tiled=True),
-        lax.all_gather(down_blocks, "fsdp", axis=1, tiled=True),
+        gather_over(down_blocks, "fsdp", 1),
     )
     gate_eff = gate_all[0] * live_blocks[0]
     up_eff = up_all[0] * live_blocks[1]

time: 608 us -> 572 us (0.941)
  waiting for transfers between devices: 426 us -> 375 us
  starting transfers between devices: 0.5 us -> 12.2 us
    all_gather x1, waiting for transfers between devices: 40.1 us -> 0.02 us  [shards(): lax.all_gather(gate_blocks, 'fsdp', axis=1, tiled=True)]
    all_to_all x0 -> x1, waiting for transfers between devices: none -> 40 us  [gather_over(): return jnp.concatenate(lax.all_to_all(outgoing, name, 0, 0), axis=dim)]
    all_gather x1 -> x0, waiting for transfers between devices: 38.1 us -> none  [shards(): lax.all_gather(down_blocks, 'fsdp', axis=1, tiled=True)]
    all_to_all x0 -> x1, starting transfers between devices: none -> 11.7 us  [gather_over(): return jnp.concatenate(lax.all_to_all(outgoing, name, 0, 0), axis=dim)]
    all_gather x1, waiting for transfers between devices: 41.1 us -> 29.4 us  [shards(): lax.all_gather(up_blocks, 'fsdp', axis=1, tiled=True)]
    unnamed x30 -> x34, local copies, waits for them, and re-layouts: 14.4 us -> 13.9 us
  transfers between devices with their start and end apart: 8 -> 8, of which waited for: 7 -> 6; matrix products, arithmetic and copies ran while one was open for 19% -> 21% of each run, Pallas kernels for 0% -> 0%
where the time goes in v1:
time: 572 us; the launch traced here: 570 us
  waiting for transfers between devices  375 us (66%)
  other arithmetic  81 us (14%)
  local copies, waits for them, and re-layouts  47.1 us (8%)
  matrix products  40.4 us (7%)
  between operations  14.4 us (3%)
  starting transfers between devices  12.2 us (2%)
    reduce_scatter x1, waiting for transfers between devices, shards(): lax.psum_scatter(up_part[None].astype(jnp.bfloat16), 'fsdp', scatter_dime...  95.9 us
    reduce_scatter x1, waiting for transfers between devices, shards(): lax.psum_scatter(down_part[None].astype(jnp.bfloat16), 'fsdp', scatter_di...  94.1 us
    reduce_scatter x1, waiting for transfers between devices, shards(): lax.psum_scatter(gate_part[None].astype(jnp.bfloat16), 'fsdp', scatter_di...  93.9 us
    scatter-add x6, other arithmetic, collect(): return jax.ops.segment_sum(block_terms, segment_ids, num_segments=segments)  67.6 us
    dot_general x9, matrix products, blockwise(): jnp.einsum(pattern, left_side, right_side, preferred_element_type=jnp.flo...  40.4 us
    all_to_all x1, waiting for transfers between devices, gather_over(): return jnp.concatenate(lax.all_to_all(outgoing, name, 0, 0), axis=dim)  40 us
    all_gather x1, waiting for transfers between devices, shards(): lax.all_gather(up_blocks, 'fsdp', axis=1, tiled=True)  29.4 us
    reduce_scatter x1, waiting for transfers between devices, shards(): lax.psum_scatter(input_term.astype(jnp.bfloat16), 'tensor', scatter_dimen...  20.3 us
  transfers between devices with their start and end apart: 8, of which 6 were waited for; matrix products, arithmetic and copies ran while one was open for 21% of the time, Pallas kernels for 0%

profile of v1, /device:TPU:2, one launch (start us, length us, event | category | flops | bytes accessed | tf_op | source)
XLA Modules:
  0.0 570.1 jit_solution(1698806312569440591)
XLA Ops:
  7.2 0.0 all-gather.3.cloned.1.call-start
  7.2 0.7 all-gather.3.cloned.1.call-update
  7.9 2.7 stack.2
  10.6 11.7 %all-to-all-start = ((bf16[32,1,2,128,128]{4,3,2,1,0:T(8,128)(2,1)}), bf16[32,1,2,128,128]{4,3,2,1,0:T(8,128)(2,1)}, u32[]{:S(2)}, u32[]{:S(2)}) async-start(bf16[32,1,2,128,128]{4,3,2,1,0:T(8,128)(2,1)} %stack.2), calls=%async_computation | async-start | bytes 4194304 | tf_op jit(solution)/shard_map/all_to_all | solution.py:11
  22.3 0.0 all-gather.5.cloned.1.call-start
  22.4 0.7 all-gather.5.cloned.1.call-update
  23.1 0.0 reduce-scatter.6.cloned.1.call-start
  23.1 2.5 copy.31
  25.6 3.2 copy.32
  29.0 2.2 gather_fusion.1
  31.2 2.1 gather_fusion
  33.3 4.1 copy.36
  37.4 3.2 copy.37
  40.7 2.2 gather_fusion.3
  42.8 0.1 fusion.14
  42.9 40.0 %all-to-all-done = bf16[32,1,2,128,128]{4,3,2,1,0:T(8,128)(2,1)} async-done(((bf16[32,1,2,128,128]{4,3,2,1,0:T(8,128)(2,1)}), bf16[32,1,2,128,128]{4,3,2,1,0:T(8,128)(2,1)}, u32[]{:S(2)}, u32[]{:S(2)}) %all-to-all-start) | async-done | bytes 2097184 | tf_op jit(solution)/shard_map/all_to_all | solution.py:11
  82.9 1.9 bitcast_multiply_fusion
  84.9 0.3 copy-done.8
  85.2 3.6 fusion.13
  88.7 0.1 broadcast.238.clone
  88.8 8.9 %scatter_fusion.3 = f32[14,128,128]{2,1,0:T(8,128)S(1)} fusion(f32[14,128,128]{2,1,0:T(8,128)S(1)} %broadcast.238.clone, s32[64]{0:T(128)S(1)} %get-tuple-element.50, f32[64,128,128]{2,1,0:T(8,128)} %fusion.13), kind=kCustom, calls=%fused_computation.9 | custom fusion | flops 1048576 | bytes 12583168 | tf_op jit(solution)/shard_map/scatter-add | solution.py:19
  97.7 0.0 all-gather.3.cloned.1.call-done
  97.7 4.4 fusion.1
  102.1 0.1 broadcast.238.clone.1
  102.2 8.8 %scatter_fusion = f32[14,128,128]{2,1,0:T(8,128)S(1)} fusion(f32[14,128,128]{2,1,0:T(8,128)S(1)} %broadcast.238.clone.1, s32[64]{0:T(128)S(1)} %get-tuple-element.52, f32[64,128,128]{2,1,0:T(8,128)} %fusion.1), kind=kCustom, calls=%fused_computation.6 | custom fusion | flops 1048576 | bytes 12583168 | tf_op jit(solution)/shard_map/scatter-add | solution.py:19
  111.0 29.4 %all-gather.5.cloned.1.call-done = bf16[1,64,128,128]{3,2,0,1:T(8,128)(2,1)} async-done(((bf16[1,2,128,128]{3,2,0,1:T(8,128)(2,1)}), bf16[1,64,128,128]{3,2,0,1:T(8,128)(2,1)}) %all-gather.5.cloned.1.call-update) | async-done | bytes 2097168 | tf_op jit(solution)/shard_map/all_gather | solution.py:44
  140.4 5.0 fusion.3
  145.3 0.1 broadcast.238.clone.2
  145.4 8.8 %scatter_fusion.1 = f32[14,128,128]{2,1,0:T(8,128)S(1)} fusion(f32[14,128,128]{2,1,0:T(8,128)S(1)} %broadcast.238.clone.2, s32[64]{0:T(128)S(1)} %get-tuple-element.53, f32[64,128,128]{2,1,0:T(8,128)} %fusion.3), kind=kCustom, calls=%fused_computation.7 | custom fusion | flops 1048576 | bytes 12583168 | tf_op jit(solution)/shard_map/scatter-add | solution.py:19
  154.2 1.6 multiply_convert_fusion.3
  155.8 3.3 gather_fusion.2
  159.1 4.3 fusion.12
  163.5 2.5 broadcast.236.clone
  165.9 13.6 %scatter_fusion.2 = f32[64,128,128]{2,1,0:T(8,128)} fusion(f32[64,128,128]{2,1,0:T(8,128)} %broadcast.236.clone, s32[64]{0:T(128)S(1)} %get-tuple-element.51, f32[64,128,128]{2,1,0:T(8,128)} %fusion.12), kind=kCustom, calls=%fused_computation.8 | custom fusion | flops 1048576 | bytes 12583168 | tf_op jit(solution)/shard_map/scatter-add | solution.py:19
  179.6 3.9 convert_element_type.63
  183.5 0.2 reduce-scatter.8.cloned.1.call-start
  183.7 0.8 copy-done.2
  184.5 2.2 gather_fusion.5
  186.7 2.2 gather_fusion.4
  188.9 5.2 fusion
  194.1 2.5 broadcast.236.clone.1
  196.6 13.8 %scatter_fusion.4 = f32[64,128,128]{2,1,0:T(8,128)} fusion(f32[64,128,128]{2,1,0:T(8,128)} %broadcast.236.clone.1, s32[64]{0:T(128)S(1)} %get-tuple-element.25, f32[64,128,128]{2,1,0:T(8,128)} %fusion), kind=kCustom, calls=%fused_computation.10 | custom fusion | flops 1048576 | bytes 12583168 | tf_op jit(solution)/shard_map/scatter-add | solution.py:19
  210.4 5.2 fusion.2
  215.6 2.5 broadcast.236.clone.2
  218.1 13.7 %scatter_fusion.5 = f32[64,128,128]{2,1,0:T(8,128)} fusion(f32[64,128,128]{2,1,0:T(8,128)} %broadcast.236.clone.2, s32[64]{0:T(128)S(1)} %get-tuple-element.19, f32[64,128,128]{2,1,0:T(8,128)} %fusion.2), kind=kCustom, calls=%fused_computation.11 | custom fusion | flops 1048576 | bytes 12583168 | tf_op jit(solution)/shard_map/scatter-add | solution.py:19
  231.8 5.8 %add_convert_fusion = bf16[64,128,128]{2,1,0:T(8,128)(2,1)} fusion(f32[64,128,128]{2,1,0:T(8,128)} %scatter_fusion.4, f32[64,128,128]{2,1,0:T(8,128)} %scatter_fusion.5), kind=kLoop, calls=%fused_computation.15 | loop fusion | flops 2097152 | bytes 10485760 | tf_op jit(solution)/shard_map/convert_element_type | solution.py:95
  237.6 0.0 reduce-scatter.12.cloned.1.call-start
  237.7 1.5 copy-done.5
  239.2 4.2 fusion.5
  243.3 0.0 reduce-scatter.10.cloned.1.call-start
  243.4 1.5 copy-done.7
  244.9 4.3 fusion.4
  249.2 0.0 reduce-scatter.14.cloned.1.call-start
  249.3 1.5 copy-done.9
  250.8 4.2 fusion.6
  255.1 0.0 reduce-scatter.6.cloned.1.call-done
  255.1 1.1 copy.35
  256.2 0.9 copy.42
  257.1 20.3 %reduce-scatter.8.cloned.1.call-done = bf16[8,128,128]{2,1,0:T(8,128)(2,1)} async-done(((bf16[64,128,128]{2,1,0:T(8,128)(2,1)}), bf16[8,128,128]{2,1,0:T(8,128)(2,1)}) %reduce-scatter.8.cloned.1.call-update) | async-done | bytes 262160 | tf_op jit(solution)/shard_map/reduce_scatter | solution.py:94
  277.3 1.1 copy.38
  278.5 0.9 copy.43
  279.3 95.9 %reduce-scatter.12.cloned.1.call-done = bf16[1,2,128,128]{3,2,1,0:T(8,128)(2,1)} async-done(((bf16[1,64,128,128]{3,2,1,0:T(8,128)(2,1)}), bf16[1,2,128,128]{3,2,1,0:T(8,128)(2,1)}) %reduce-scatter.12.cloned.1.call-update) | async-done | bytes 65552 | tf_op jit(solution)/shard_map/reduce_scatter | solution.py:87
  375.2 93.9 %reduce-scatter.10.cloned.1.call-done = bf16[1,2,128,128]{3,2,1,0:T(8,128)(2,1)} async-done(((bf16[1,64,128,128]{3,2,1,0:T(8,128)(2,1)}), bf16[1,2,128,128]{3,2,1,0:T(8,128)(2,1)}) %reduce-scatter.10.cloned.1.call-update) | async-done | bytes 65552 | tf_op jit(solution)/shard_map/reduce_scatter | solution.py:84
  469.1 94.1 %reduce-scatter.14.cloned.1.call-done = bf16[1,2,128,128]{3,2,1,0:T(8,128)(2,1)} async-done(((bf16[1,64,128,128]{3,2,1,0:T(8,128)(2,1)}), bf16[1,2,128,128]{3,2,1,0:T(8,128)(2,1)}) %reduce-scatter.14.cloned.1.call-update) | async-done | bytes 65552 | tf_op jit(solution)/shard_map/reduce_scatter | solution.py:90
  (41 shorter events, 0.3 us)
Async XLA Ops:
  7.2 90.6 %all-gather.3.cloned.1.call-start = ((), (), s32[]{:S(2)}) async-start(), calls=%async_computation.6 | async-start | bytes 2162688 | tf_op jit(solution)/shard_map/all_gather | solution.py:43
  10.6 12.6 %copy-start.10 = (bf16[128,8192]{1,0:T(8,128)(2,1)S(1)}, bf16[128,8192]{1,0:T(8,128)(2,1)}, u32[]{:S(2)}) copy-start(bf16[128,8192]{1,0:T(8,128)(2,1)} %param.13) | copy-start | bytes 6291460
  10.6 72.4 %all-to-all-start = ((bf16[32,1,2,128,128]{4,3,2,1,0:T(8,128)(2,1)}), bf16[32,1,2,128,128]{4,3,2,1,0:T(8,128)(2,1)}, u32[]{:S(2)}, u32[]{:S(2)}) async-start(bf16[32,1,2,128,128]{4,3,2,1,0:T(8,128)(2,1)} %stack.2), calls=%async_computation | async-start | bytes 4194304 | tf_op jit(solution)/shard_map/all_to_all | solution.py:11
  22.3 118.1 %all-gather.5.cloned.1.call-start = ((), (), s32[]{:S(2)}) async-start(), calls=%async_computation.7 | async-start | bytes 2162688 | tf_op jit(solution)/shard_map/all_gather | solution.py:44
  23.1 232.0 %reduce-scatter.6.cloned.1.call-start = ((), (), s32[]{:S(2)}) async-start(), calls=%async_computation.8 | async-start | bytes 2359296 | tf_op jit(solution)/shard_map/reduce_scatter | solution.py:66
  25.6 3.2 copy-start.11
  28.9 2.2 copy-start.12
  37.4 3.2 copy-start.13
  40.6 2.2 copy-start.14
  82.9 2.2 copy-start.8
  84.9 3.8 copy-start
  88.8 8.9 %copy-start.6 = (bf16[64,128,128]{2,1,0:T(8,128)(2,1)S(1)}, bf16[64,128,128]{2,1,0:T(8,128)(2,1)}, u32[]{:S(2)}) copy-start(bf16[64,128,128]{2,1,0:T(8,128)(2,1)} %gather_fusion) | copy-start | bytes 6291460
  155.8 3.3 copy-start.1
  183.5 1.0 copy-start.2
  183.5 93.8 %reduce-scatter.8.cloned.1.call-start = ((), (), s32[]{:S(2)}) async-start(), calls=%async_computation.9 | async-start | bytes 2359296 | tf_op jit(solution)/shard_map/reduce_scatter | solution.py:94
  186.7 2.2 copy-start.3
  196.6 13.8 %copy-start.4 = (bf16[1,64,128,128]{3,2,0,1:T(8,128)(2,1)S(1)}, bf16[1,64,128,128]{3,2,0,1:T(8,128)(2,1)}, u32[]{:S(2)}) copy-start(bf16[1,64,128,128]{3,2,0,1:T(8,128)(2,1)} %all-gather.5.cloned.1.call-done) | copy-start | bytes 6291460
  237.6 1.6 copy-start.5
  237.6 137.6 %reduce-scatter.12.cloned.1.call-start = ((), (), s32[]{:S(2)}) async-start(), calls=%async_computation.11 | async-start | bytes 2162688 | tf_op jit(solution)/shard_map/reduce_scatter | solution.py:87
  243.3 1.6 copy-start.7
  243.3 225.8 %reduce-scatter.10.cloned.1.call-start = ((), (), s32[]{:S(2)}) async-start(), calls=%async_computation.10 | async-start | bytes 2162688 | tf_op jit(solution)/shard_map/reduce_scatter | solution.py:84
  249.2 1.6 copy-start.9
  249.2 314.0 %reduce-scatter.14.cloned.1.call-start = ((), (), s32[]{:S(2)}) async-start(), calls=%async_computation.12 | async-start | bytes 2162688 | tf_op jit(solution)/shard_map/reduce_scatter | solution.py:90
Sparse Core Ops, SparseCore 0:
  10.5 73.1 all-gather.2
  86.3 54.0 all-gather.4
  183.6 39.7 reduce-scatter.5
  237.7 39.5 reduce-scatter.7
  281.6 93.5 reduce-scatter.11
  379.5 89.6 reduce-scatter.9
  473.5 89.6 reduce-scatter.13
